TPU v7x, 32 devices: a whole 2x2x4 slice. The times are simulated.
32 devices in a mesh: cuts: 4 (over z), fsdp: 8 (over y, x, core).
Axes of the slice: x: 2, y: 2, z: 4, core: 2. Of those that a mesh axis runs over, the one named last changes fastest.
Arguments:
- tokens: bfloat16 [4096, 8192], P(('cuts', 'fsdp')), may hold values from -240 to 240
- norm_gain: bfloat16 [8192], P('fsdp'), may hold values from 0.5 to 1.5
- gate_weight: bfloat16 [8192, 256], P('fsdp'), may hold values from -0.0625 to 0.0625
- up_weight: bfloat16 [8192, 256], P('fsdp'), may hold values from -0.0625 to 0.0625
- down_weight: bfloat16 [256, 8192], P(None, 'fsdp'), may hold values from -0.375 to 0.375
- slice_grads: float32 [4, 3, 8192, 256], P('cuts', None, 'fsdp'), may hold values from -6 to 6
Outputs:
- branch_out: bfloat16 [4096, 8192], P(('cuts', 'fsdp'))
- grad_mean: float32 [3, 8192, 256], P(None, 'fsdp')
All inputs are finite; a program needn't handle non-finite values.
Results may differ from a plain program's by a relative error of at most 0.0065.
Values may be sent and summed in bfloat16 or wider, within the bound.
A program may use at most 64 MiB of HBM per device.

v0:
```python
import jax
import jax.numpy as jnp
from jax import lax
from jax.sharding import PartitionSpec as P


def average_grads(slice_grads):
    summed = lax.psum(slice_grads[0], "cuts")
    return summed / lax.axis_size("cuts")


def per_device(tokens, norm_gain, gate_weight, up_weight, down_weight, slice_grads):
    tok_float = tokens.astype(jnp.float32)
    inv_rms = lax.rsqrt(jnp.mean(tok_float * tok_float, axis=1, keepdims=True) + 1e-05)
    gathered = (
        lax.all_gather(gate_weight, "fsdp", axis=0, tiled=True),
        lax.all_gather(up_weight, "fsdp", axis=0, tiled=True),
        lax.all_gather(norm_gain, "fsdp", axis=0, tiled=True),
    )
    normed = (tok_float * inv_rms * gathered[2].astype(jnp.float32)[None, :]).astype(jnp.bfloat16)
    gate_out = jnp.dot(normed, gathered[0], preferred_element_type=jnp.float32)
    up_out = jnp.dot(normed, gathered[1], preferred_element_type=jnp.float32)
    hidden = (jax.nn.silu(gate_out) * up_out).astype(jnp.bfloat16)
    down_full = lax.all_gather(down_weight, "fsdp", axis=1, tiled=True)
    branch = jnp.dot(hidden, down_full, preferred_element_type=jnp.float32)
    grad_mean = average_grads(slice_grads)
    return (branch.astype(jnp.bfloat16), grad_mean)


def solution(mesh):
    return jax.shard_map(
        per_device,
        mesh=mesh,
        in_specs=(
            P(("cuts", "fsdp"), None),
            P("fsdp"),
            P("fsdp", None),
            P("fsdp", None),
            P(None, "fsdp"),
            P("cuts", None, "fsdp", None),
        ),
        out_specs=(P(("cuts", "fsdp"), None), P(None, "fsdp", None)),
        check_vma=False,
    )
```

profile of v0, /device:TPU:0, one launch (start us, length us, event | category | flops | bytes accessed | tf_op | source)
XLA Modules:
  0.0 156.7 jit_solution(2685609127519770182)
XLA Ops:
  8.0 0.0 copy-start.1
  8.0 0.0 copy-start
  8.0 0.0 all-reduce.2.cloned.1.call-start
  8.1 0.7 all-reduce.2.cloned.1.call-update
  8.8 0.0 all-gather.4.cloned.1.call-start
  8.8 0.5 all-gather.4.cloned.1.call-update
  9.3 0.0 all-gather.6.cloned.1.call-start
  9.4 0.5 all-gather.6.cloned.1.call-update
  9.9 0.0 all-gather.8.cloned.1.call-start
  10.0 0.5 all-gather.8.cloned.1.call-update
  10.5 0.0 copy-done.1
  10.5 10.4 %all_gather.12 = bf16[8192]{0:T(1024)(128)(2,1)S(1)} all-gather(bf16[1024]{0:T(1024)(128)(2,1)S(1)} %copy-done.1), channel_id=1, replica_groups=mesh['cuts'=4,'fsdp'=8] {'fsdp'}, dimensions={0}, use_global_device_ids=true | all-gather | bytes 18432 | tf_op jit(solution)/shard_map/all_gather | solution.py:18
  20.9 0.0 copy-done
  20.9 0.5 fusion
  21.4 113.6 %all-reduce.2.cloned.1.call-done = f32[3,1024,256]{2,1,0:T(8,128)} async-done(((f32[3,1024,256]{2,1,0:T(8,128)}), f32[3,1024,256]{2,1,0:T(8,128)}) %all-reduce.2.cloned.1.call-update) | async-done | bytes 3145744 | tf_op jit(solution)/shard_map/psum | solution.py:8
  135.0 3.8 %broadcast_multiply_fusion = f32[3,1024,256]{2,1,0:T(8,128)} fusion(f32[3,1024,256]{2,1,0:T(8,128)} %all-reduce.2.cloned.1.call-done), kind=kLoop, calls=%fused_computation.6 | loop fusion | flops 786432 | bytes 6291456 | tf_op jit(solution)/shard_map/div | solution.py:9
  138.8 0.0 all-gather.4.cloned.1.call-done
  138.8 2.9 %fusion.6 = f32[128,256]{1,0:T(8,128)S(1)} fusion(bf16[8192,256]{1,0:T(8,128)(2,1)} %all-gather.4.cloned.1.call-done, bf16[128,8192]{1,0:T(8,128)(2,1)S(1)} %copy-done, f32[8192]{0:T(1024)S(1)} %convert_element_type.16, f32[128]{0:T(128)S(1)} %add_rsqrt_fusion), kind=kOutput, calls=%fused_computation.9 | convolution fusion | flops 541065216 | bytes 6455808 | tf_op jit(solution)/shard_map/dot_general | solution.py:21
  141.8 0.0 all-gather.6.cloned.1.call-done
  141.8 0.0 all-gather.8.cloned.1.call-done
  141.8 7.2 %convolution_convert_fusion = bf16[128,8192]{1,0:T(8,128)(2,1)} fusion(bf16[256,8192]{1,0:T(8,128)(2,1)} %all-gather.8.cloned.1.call-done, bf16[8192,256]{1,0:T(8,128)(2,1)} %all-gather.6.cloned.1.call-done, bf16[128,8192]{1,0:T(8,128)(2,1)S(1)} %copy-done, f32[8192]{0:T(1024)S(1)} %convert_element_type.16, f32[128]{0:T(128)S(1)} %add_rsqrt_fusion, ...), kind=kOutput, calls=%fused_computation | convolution fusion | flops 1079181312 | bytes 12747264 | tf_op jit(solution)/shard_map/dot_general | solution.py:25
  (2 shorter events, 0.0 us)
Async XLA Ops:
  8.0 2.5 %copy-start.1 = (bf16[1024]{0:T(1024)(128)(2,1)S(1)}, bf16[1024]{0:T(1024)(128)(2,1)}, u32[]{:S(2)}) copy-start(bf16[1024]{0:T(1024)(128)(2,1)} %param.7) | copy-start | bytes 6148
  8.0 12.9 %copy-start = (bf16[128,8192]{1,0:T(8,128)(2,1)S(1)}, bf16[128,8192]{1,0:T(8,128)(2,1)}, u32[]{:S(2)}) copy-start(bf16[128,8192]{1,0:T(8,128)(2,1)} %param.6) | copy-start | bytes 6291460
  8.0 127.0 %all-reduce.2.cloned.1.call-start = ((), (), s32[]{:S(2)}) async-start(), calls=%async_computation.3 | async-start | bytes 6291456 | tf_op jit(solution)/shard_map/psum | solution.py:8
  8.8 130.1 %all-gather.4.cloned.1.call-start = ((), (), s32[]{:S(2)}) async-start(), calls=%async_computation | async-start | bytes 4718592 | tf_op jit(solution)/shard_map/all_gather | solution.py:16
  9.3 132.5 %all-gather.6.cloned.1.call-start = ((), (), s32[]{:S(2)}) async-start(), calls=%async_computation.1 | async-start | bytes 4718592 | tf_op jit(solution)/shard_map/all_gather | solution.py:17
  9.9 131.9 %all-gather.8.cloned.1.call-start = ((), (), s32[]{:S(2)}) async-start(), calls=%async_computation.2 | async-start | bytes 4718592 | tf_op jit(solution)/shard_map/all_gather | solution.py:24
Sparse Core Ops, SparseCore 0:
  11.2 123.7 all-reduce.1
Sparse Core Ops, SparseCore 1:
  11.1 39.2 all-gather.3
  52.1 36.4 all-gather.5
  90.4 36.4 all-gather.7
where the time goes:
time: 157 us
  waiting for transfers between devices  116 us (74%)
  between operations  15.7 us (10%)
  blocking collectives  10.4 us (7%)
  matrix products  10.2 us (6%)
  other arithmetic  4.32 us (3%)
    psum x1, waiting for transfers between devices, average_grads(): summed = lax.psum(slice_grads[0], 'cuts')  114 us
    all_gather x1, blocking collectives, per_device(): lax.all_gather(norm_gain, 'fsdp', axis=0, tiled=True)  10.4 us
    dot_general x1, matrix products, per_device(): branch = jnp.dot(hidden, down_full, preferred_element_type=jnp.float32)  7.24 us
    div x1, other arithmetic, average_grads(): return summed / lax.axis_size('cuts')  3.82 us
  transfers between devices with their start and end apart: 4, of which 1 were waited for; matrix products, arithmetic and copies ran while one was open for 5% of the time, Pallas kernels for 0%

commit v1 on v0

--- a/solution.py
+++ b/solution.py
@@ -4,8 +4,13 @@
 from jax.sharding import PartitionSpec as P
 
 
+def choose_row(body):
+    mixed_arr = lax.all_gather(body, axis_name="cuts")
+    return jnp.sum(mixed_arr, 0)
+
+
 def average_grads(slice_grads):
-    summed = lax.psum(slice_grads[0], "cuts")
+    summed = choose_row(slice_grads[0])
     return summed / lax.axis_size("cuts")
 
 

time: 157 us -> 360 us (2.29)
  waiting for transfers between devices: 116 us -> 317 us
  other arithmetic: 4.32 us -> 8.25 us
    all_gather x0 -> x1, waiting for transfers between devices: none -> 212 us  [choose_row(): mixed_arr = lax.all_gather(body, axis_name='cuts')]
    psum x1 -> x0, waiting for transfers between devices: 114 us -> none  [average_grads(): summed = lax.psum(slice_grads[0], 'cuts')]
    all_gather x1, waiting for transfers between devices: 0.02 us -> 38.5 us  [per_device(): down_full = lax.all_gather(down_weight, 'fsdp', axis=1, tiled=True)]
    all_gather x1, waiting for transfers between devices: 0.03 us -> 35.6 us  [per_device(): lax.all_gather(up_weight, 'fsdp', axis=0, tiled=True)]
    all_gather x1, waiting for transfers between devices: 0.01 us -> 28.3 us  [per_device(): lax.all_gather(gate_weight, 'fsdp', axis=0, tiled=True)]
    reduce_sum x0 -> x1, other arithmetic: none -> 5.82 us  [choose_row(): return jnp.sum(mixed_arr, 0)]
  transfers between devices with their start and end apart: 4 -> 4, of which waited for: 1 -> 4; matrix products, arithmetic and copies ran while one was open for 5% -> 3% of each run, Pallas kernels for 0% -> 0%
where the time goes in v1:
time: 360 us
  waiting for transfers between devices  317 us (88%)
  between operations  13.8 us (4%)
  blocking collectives  10.4 us (3%)
  matrix products  10.2 us (3%)
  other arithmetic  8.25 us (2%)
    all_gather x1, waiting for transfers between devices, choose_row(): mixed_arr = lax.all_gather(body, axis_name='cuts')  212 us
    all_gather x1, waiting for transfers between devices, per_device(): down_full = lax.all_gather(down_weight, 'fsdp', axis=1, tiled=True)  38.5 us
    all_gather x1, waiting for transfers between devices, per_device(): lax.all_gather(up_weight, 'fsdp', axis=0, tiled=True)  35.6 us
    all_gather x1, waiting for transfers between devices, per_device(): lax.all_gather(gate_weight, 'fsdp', axis=0, tiled=True)  28.3 us
    all_gather x1, blocking collectives, per_device(): lax.all_gather(norm_gain, 'fsdp', axis=0, tiled=True)  10.4 us
    dot_general x1, matrix products, per_device(): branch = jnp.dot(hidden, down_full, preferred_element_type=jnp.float32)  7.23 us
  transfers between devices with their start and end apart: 4, of which 4 were waited for; matrix products, arithmetic and copies ran while one was open for 3% of the time, Pallas kernels for 0%

profile of v1, /device:TPU:0, one launch (start us, length us, event | category | flops | bytes accessed | tf_op | source)
XLA Modules:
  0.0 360.2 jit_solution(14441288608573569151)
XLA Ops:
  7.2 0.0 copy-start.1
  7.2 0.0 copy-start
  7.2 0.0 all-gather.5.cloned.1.call-start
  7.2 0.7 all-gather.5.cloned.1.call-update
  7.9 0.0 all-gather.7.cloned.1.call-start
  8.0 0.7 all-gather.7.cloned.1.call-update
  8.7 0.0 all-gather.9.cloned.1.call-start
  8.7 0.7 all-gather.9.cloned.1.call-update
  9.4 0.0 all-gather.11.cloned.1.call-start
  9.4 0.5 all-gather.11.cloned.1.call-update
  10.0 0.0 copy-done.1
  10.0 10.4 %all_gather.15 = bf16[8192]{0:T(1024)(128)(2,1)S(1)} all-gather(bf16[1024]{0:T(1024)(128)(2,1)S(1)} %copy-done.1), channel_id=1, replica_groups=mesh['cuts'=4,'fsdp'=8] {'fsdp'}, dimensions={0}, use_global_device_ids=true | all-gather | bytes 18432 | tf_op jit(solution)/shard_map/all_gather | solution.py:23
  20.4 0.0 copy-done
  20.4 0.5 fusion
  20.9 28.3 %all-gather.5.cloned.1.call-done = bf16[8192,256]{1,0:T(8,128)(2,1)} async-done(((bf16[1024,256]{1,0:T(8,128)(2,1)}), bf16[8192,256]{1,0:T(8,128)(2,1)}) %all-gather.5.cloned.1.call-update) | async-done | bytes 4194320 | tf_op jit(solution)/shard_map/all_gather | solution.py:21
  49.2 2.9 fusion.6
  52.2 35.6 %all-gather.7.cloned.1.call-done = bf16[8192,256]{1,0:T(8,128)(2,1)} async-done(((bf16[1024,256]{1,0:T(8,128)(2,1)}), bf16[8192,256]{1,0:T(8,128)(2,1)}) %all-gather.7.cloned.1.call-update) | async-done | bytes 4194320 | tf_op jit(solution)/shard_map/all_gather | solution.py:22
  87.7 38.5 %all-gather.9.cloned.1.call-done = bf16[256,8192]{1,0:T(8,128)(2,1)} async-done(((bf16[256,1024]{1,0:T(8,128)(2,1)}), bf16[256,8192]{1,0:T(8,128)(2,1)}) %all-gather.9.cloned.1.call-update) | async-done | bytes 4194320 | tf_op jit(solution)/shard_map/all_gather | solution.py:29
  126.2 7.2 %convolution_convert_fusion = bf16[128,8192]{1,0:T(8,128)(2,1)} fusion(bf16[256,8192]{1,0:T(8,128)(2,1)} %all-gather.9.cloned.1.call-done, bf16[8192,256]{1,0:T(8,128)(2,1)} %all-gather.7.cloned.1.call-done, bf16[128,8192]{1,0:T(8,128)(2,1)S(1)} %copy-done, f32[8192]{0:T(1024)S(1)} %convert_element_type.16, f32[128]{0:T(128)S(1)} %add_rsqrt_fusion, ...), kind=kOutput, calls=%fused_computation | convolution fusion | flops 1079181312 | bytes 12747264 | tf_op jit(solution)/shard_map/dot_general | solution.py:30
  133.5 212.4 %all-gather.11.cloned.1.call-done = f32[4,3,1024,256]{3,2,1,0:T(8,128)} async-done(((f32[1,3,1024,256]{3,2,1,0:T(8,128)}), f32[4,3,1024,256]{3,2,1,0:T(8,128)}) %all-gather.11.cloned.1.call-update) | async-done | bytes 12582928 | tf_op jit(solution)/shard_map/all_gather | solution.py:8
  345.9 5.8 %reduce_sum.19 = f32[3,1024,256]{2,1,0:T(8,128)S(1)} reduce(f32[4,3,1024,256]{3,2,1,0:T(8,128)} %all-gather.11.cloned.1.call-done, f32[]{:T(128)} %constant.3.clone.1), dimensions={0}, to_apply=%region_1.2 | reduce | flops 2359296 | bytes 15728644 | tf_op jit(solution)/shard_map/reduce_sum | solution.py:9
  351.7 1.9 broadcast_multiply_fusion
  (2 shorter events, 0.0 us)
Async XLA Ops:
  7.2 2.8 copy-start.1
  7.2 13.2 %copy-start = (bf16[128,8192]{1,0:T(8,128)(2,1)S(1)}, bf16[128,8192]{1,0:T(8,128)(2,1)}, u32[]{:S(2)}) copy-start(bf16[128,8192]{1,0:T(8,128)(2,1)} %param.6) | copy-start | bytes 6291460
  7.2 42.0 %all-gather.5.cloned.1.call-start = ((), (), s32[]{:S(2)}) async-start(), calls=%async_computation | async-start | bytes 4718592 | tf_op jit(solution)/shard_map/all_gather | solution.py:21
  7.9 79.8 %all-gather.7.cloned.1.call-start = ((), (), s32[]{:S(2)}) async-start(), calls=%async_computation.1 | async-start | bytes 4718592 | tf_op jit(solution)/shard_map/all_gather | solution.py:22
  8.7 117.6 %all-gather.9.cloned.1.call-start = ((), (), s32[]{:S(2)}) async-start(), calls=%async_computation.2 | async-start | bytes 4718592 | tf_op jit(solution)/shard_map/all_gather | solution.py:29
  9.4 336.5 %all-gather.11.cloned.1.call-start = ((), (), s32[]{:S(2)}) async-start(), calls=%async_computation.3 | async-start | bytes 15728640 | tf_op jit(solution)/shard_map/all_gather | solution.py:8
Sparse Core Ops, SparseCore 0:
  9.9 39.2 all-gather.4
  51.1 36.5 all-gather.6
  89.6 36.5 all-gather.8
  127.7 218.1 all-gather.10
